TPU v7x, 256 devices: a whole 4x4x8 slice. The times are simulated.
256 devices in a mesh: dp: 16 (over x, y_lo, core), blk: 16 (over y_hi, z).
Axes of the slice: x: 4, y: 4 (y_hi: 2, y_lo: 2; y = y_hi * 2 + y_lo), z: 8, core: 2. Of those that a mesh axis runs over, the one named last changes fastest.
Arguments:
- layer_input: bfloat16 [16, 4096, 2048], P('dp', 'blk'), may hold values from -6 to 6
- queries: bfloat16 [16, 4096, 1024], P('dp', 'blk'), may hold values from -28 to 28
- key_rows: bfloat16 [16, 4096, 1024], P('dp', 'blk'), may hold values from -4 to 4
- value_rows: bfloat16 [16, 4096, 1024], P('dp', 'blk'), may hold values from -6 to 6
- context: bfloat16 [16, 4096, 1024], P('dp', 'blk'), may hold values from -6 to 6
- grad_context: bfloat16 [16, 4096, 1024], P('dp', 'blk'), may hold values from -6 to 6
- grad_output: bfloat16 [16, 4096, 2048], P('dp', 'blk'), may hold values from -6 to 6
- earlier_mass: float32 [16, 4, 4096], P('dp', None, 'blk'), may hold values from 3 to 7
- grad_queries: float32 [16, 4096, 1024], P('dp', 'blk'), may hold values from -0.12 to 0.12
- grad_keys: float32 [16, 4096, 1024], P('dp', 'blk'), may hold values from -0.12 to 0.12
- grad_values: float32 [16, 4096, 1024], P('dp', 'blk'), may hold values from -0.12 to 0.12
- documents: int32 [16, 4096], P('dp', 'blk'), may hold values from 0 to 2, as said below
- weights: float32 [4, 2048, 1024], P(None, 'blk', 'dp'), may hold values from -0.125 to 0.125
- row_factor: float32 [4, 2048], P(None, 'blk'), may hold values from 1.525879e-08 to 1.5258789e-05
- column_factor: float32 [4, 1024], P(None, 'dp'), may hold values from 1.525879e-08 to 1.5258789e-05
Outputs:
- new_weights: float32 [4, 2048, 1024], P(None, 'blk', 'dp')
- new_row_factor: float32 [4, 2048], P(None, 'blk')
- new_column_factor: float32 [4, 1024], P(None, 'dp')
Inputs may be any that keep to these rules, and one draw needn't show every extreme that they name: Read in order of position, a sequence's document numbers never fall; each sequence has three documents of 512 positions or more.
All inputs are finite; a program needn't handle non-finite values.
Results may differ from a plain program's by a relative error of at most 0.022.
Values may be sent and summed in bfloat16 or wider, within the bound.
A program may use at most 128 MiB of HBM per device.

v0:
```python
import math

import jax
import jax.numpy as jnp
from jax import lax
from jax.sharding import PartitionSpec as P

beta_two = 0.9
learn_rate = 0.05
tiny_square = 1e-30


def passed_along(value, axis, steps):
    count = lax.axis_size(axis)
    pairs = [(source, (source + steps) % count) for source in range(count)]
    return lax.ppermute(value, axis, pairs)


def as_sent(array):
    return jax.tree.map(lambda a: a.astype(jnp.bfloat16) if a.dtype == jnp.float32 else a, array)


def in_blocks(array, dim, devices):
    before, after = (array.shape[:dim], array.shape[dim + 1 :])
    return jnp.moveaxis(array.reshape(*before, devices, -1, *after), dim, 0)


def sum_at_owner(array, axis, dim):
    devices = lax.axis_size(axis)
    pieces = lax.all_to_all(in_blocks(array, dim, devices), axis, 0, 0, tiled=True)
    return jnp.sum(pieces.astype(jnp.float32), axis=0)


def from_everyone(array, axis):
    devices = lax.axis_size(axis)
    return lax.all_to_all(
        jnp.broadcast_to(array[None], (devices, *array.shape)), axis, 0, 0, tiled=True
    )


def taken_together(array, axis):
    everything = from_everyone(array, axis)
    return jnp.sum(everything, axis=0)


def folded_rows(block_index, blocks, row_count):
    half = row_count // 2
    local = jnp.arange(row_count, dtype=jnp.int32)
    lower = block_index * half + local
    upper = (2 * blocks - 1 - block_index) * half + local - half
    return jnp.where(local < half, lower, upper)


def attend_back(queries, key_rows, value_rows, context, grad_context, earlier_mass, allowed):
    row_count = queries.shape[0]
    key_count = key_rows.shape[0]
    head_count = earlier_mass.shape[0]
    head_size = queries.shape[1] // head_count
    scale_factor = 1.0 / math.sqrt(head_size)
    query_heads = queries.reshape(row_count, head_count, head_size)
    key_heads = key_rows.reshape(key_count, head_count, head_size)
    value_heads = value_rows.reshape(key_count, head_count, head_size)
    context_heads = context.reshape(row_count, head_count, head_size)
    grad_heads = grad_context.reshape(row_count, head_count, head_size)
    scores = (
        jnp.einsum("thd,shd->hts", query_heads, key_heads, preferred_element_type=jnp.float32)
        * scale_factor
    )
    open_pairs = allowed[None]
    peak_score = jnp.maximum(earlier_mass, jnp.max(jnp.where(open_pairs, scores, -jnp.inf), axis=2))
    shifted = jnp.where(open_pairs, jnp.exp(scores - peak_score[:, :, None]), 0.0)
    total_mass = jnp.exp(earlier_mass - peak_score) + jnp.sum(shifted, axis=2)
    log_norm = peak_score + jnp.log(total_mass)
    attention = jnp.where(open_pairs, jnp.exp(scores - log_norm[:, :, None]), 0.0)
    attention_low = attention.astype(jnp.bfloat16)
    row_dot = jnp.sum(context_heads.astype(jnp.float32) * grad_heads.astype(jnp.float32), axis=2).T
    grad_attention = jnp.einsum(
        "thd,shd->hts", grad_heads, value_heads, preferred_element_type=jnp.float32
    )
    grad_scores = (attention * (grad_attention - row_dot[:, :, None]) * scale_factor).astype(
        jnp.bfloat16
    )
    query_step = jnp.einsum(
        "hts,shd->thd", grad_scores, key_heads, preferred_element_type=jnp.float32
    ).reshape(row_count, -1)
    key_step = jnp.einsum(
        "hts,thd->shd", grad_scores, query_heads, preferred_element_type=jnp.float32
    ).reshape(key_count, -1)
    value_step = jnp.einsum(
        "hts,thd->shd", attention_low, grad_heads, preferred_element_type=jnp.float32
    ).reshape(key_count, -1)
    return (query_step, key_step, value_step)


def body(
    layer_input,
    queries,
    key_rows,
    value_rows,
    context,
    grad_context,
    grad_output,
    earlier_mass,
    grad_queries,
    grad_keys,
    grad_values,
    documents,
    weights,
    row_factor,
    column_factor,
):
    blocks = lax.axis_size("blk")
    data_count = lax.axis_size("dp")
    block_index = lax.axis_index("blk")
    row_count = queries.shape[1]
    own_docs = documents[0]
    doc_float = own_docs.astype(jnp.bfloat16)

    def fetch_next(held):
        return passed_along((held[0], held[1], held[2]), "blk", -1)

    nearer = fetch_next((key_rows[0], value_rows[0], doc_float))
    further = fetch_next(nearer)
    seen_keys = jnp.concatenate([nearer[0], further[0]], axis=0)
    seen_values = jnp.concatenate([nearer[1], further[1]], axis=0)
    seen_docs = jnp.concatenate([nearer[2], further[2]], axis=0).astype(jnp.int32)
    own_pos = folded_rows(block_index, blocks, row_count)
    near_pos = folded_rows((block_index + 1) % blocks, blocks, row_count)
    far_pos = folded_rows((block_index + 2) % blocks, blocks, row_count)
    seen_pos = jnp.concatenate([near_pos, far_pos], axis=0)
    allowed = (seen_pos[None, :] <= own_pos[:, None]) & (seen_docs[None, :] == own_docs[:, None])
    query_step, key_step, value_step = attend_back(
        queries[0], seen_keys, seen_values, context[0], grad_context[0], earlier_mass[0], allowed
    )
    near_part = (key_step[:row_count], value_step[:row_count])
    far_part = (key_step[row_count:], value_step[row_count:])

    def send_back(pair):
        return passed_along((as_sent(pair[0]), as_sent(pair[1])), "blk", 1)

    moved = send_back(far_part)
    home = send_back((moved[0] + near_part[0], moved[1] + near_part[1]))
    query_total = grad_queries[0] + query_step
    key_total = grad_keys[0] + home[0]
    value_total = grad_values[0] + home[1]
    right_low = jnp.stack([query_total, key_total, value_total], axis=1).astype(jnp.bfloat16)
    layer_rows = layer_input[0]
    output_rows = grad_output[0]
    context_rows = context[0]
    all_tokens = data_count * blocks * row_count
    part_inner = jnp.einsum(
        "twh,td->hwd", right_low, layer_rows, preferred_element_type=jnp.float32
    )
    part_output = jnp.einsum(
        "th,td->hd", context_rows, output_rows, preferred_element_type=jnp.float32
    )
    summed = lax.psum_scatter(
        jnp.concatenate([part_inner, part_output[:, None, :]], axis=1).astype(jnp.bfloat16),
        "dp",
        scatter_dimension=0,
        tiled=True,
    )
    grouped = sum_at_owner(summed, "blk", 2)
    gradient = jnp.transpose(grouped, (1, 2, 0)) / all_tokens
    local_rows = gradient.shape[1]
    local_cols = gradient.shape[2]
    full_rows = local_rows * blocks
    full_cols = local_cols * data_count
    squares = gradient * gradient + tiny_square
    row_part = jnp.sum(squares, axis=2)
    col_part = jnp.sum(squares, axis=1)
    row_sum = taken_together(row_part, "dp")
    col_sum = taken_together(col_part, "blk")
    new_row_factor = beta_two * row_factor + (1.0 - beta_two) * row_sum / full_cols
    new_column_factor = beta_two * column_factor + (1.0 - beta_two) * col_sum / full_rows
    row_mean = taken_together(jnp.sum(new_row_factor, axis=1), "blk") / full_rows
    second = new_row_factor[:, :, None] * new_column_factor[:, None, :] / row_mean[:, None, None]
    new_weights = weights - learn_rate * gradient * lax.rsqrt(second)
    return (new_weights, new_row_factor, new_column_factor)


def solution(mesh):
    placed = (
        P("dp", "blk", None),
        P("dp", "blk", None),
        P("dp", "blk", None),
        P("dp", "blk", None),
        P("dp", "blk", None),
        P("dp", "blk", None),
        P("dp", "blk", None),
        P("dp", None, "blk"),
        P("dp", "blk", None),
        P("dp", "blk", None),
        P("dp", "blk", None),
        P("dp", "blk"),
        P(None, "blk", "dp"),
        P(None, "blk"),
        P(None, "dp"),
    )
    return jax.shard_map(
        body,
        mesh=mesh,
        in_specs=placed,
        out_specs=(P(None, "blk", "dp"), P(None, "blk"), P(None, "dp")),
        check_vma=False,
    )
```

profile of v0, /device:TPU:1, one launch (start us, length us, event | category | flops | bytes accessed | tf_op | source)
XLA Modules:
  0.0 402.0 jit_solution(13727060800298819416)
XLA Ops:
  7.2 0.8 convert_element_type.64
  8.1 9.0 %collective-permute-start.2 = (bf16[256]{0:T(256)(128)(2,1)S(1)}, bf16[256]{0:T(256)(128)(2,1)S(1)}, u32[]{:S(2)}, u32[]{:S(2)}) collective-permute-start(bf16[256]{0:T(256)(128)(2,1)S(1)} %convert_element_type.64), channel_id=1, source_target_pairs={{0,15},{1,0},{2,1},{3,2},{4,3},{5,4},{6,5},{7,6},{8,7},{9,8},{10,9... | collective-permute-start | bytes 1544 | tf_op jit(solution)/shard_map/ppermute | solution.py:16
  17.1 2.1 copy.78
  19.9 2.0 copy.81
  23.9 4.5 %convert_bitcast_fusion.1 = bf16[1024,1,2048]{2,0,1:T(8,128)(2,1)} fusion(bf16[1,256,2048]{2,1,0:T(8,128)(2,1)} %param.21, bf16[1,256,1024]{2,1,0:T(8,128)(2,1)S(1)} %copy-done.6), kind=kOutput, calls=%fused_computation.2 | convolution fusion | flops 1075838976 | bytes 5767168 | tf_op jit(solution)/shard_map/th,td->hd/dot_general | solution.py:154
  28.4 3.6 collective-permute-done
  32.0 4.3 %collective-permute-start.1 = (bf16[256,1024]{0,1:T(8,128)(2,1)}, bf16[256,1024]{0,1:T(8,128)(2,1)}, u32[]{:S(2)}, u32[]{:S(2)}) collective-permute-start(bf16[256,1024]{0,1:T(8,128)(2,1)} %collective-permute-done), channel_id=1, source_target_pairs={{0,15},{1,0},{2,1},{3,2},{4,3},{5,4},{6,5},{7,6},{8,7},{9,8},{10,9... | collective-permute-start | bytes 1572872 | tf_op jit(solution)/shard_map/ppermute | solution.py:16
  36.4 1.2 copy.91
  37.5 1.0 copy.104
  38.6 1.6 copy.86
  40.2 1.4 copy.77
  41.6 1.6 copy.89
  43.2 11.3 %collective-permute-done.3 = bf16[256]{0:T(256)(128)(2,1)S(1)} collective-permute-done((bf16[256]{0:T(256)(128)(2,1)S(1)}, bf16[256]{0:T(256)(128)(2,1)S(1)}, u32[]{:S(2)}, u32[]{:S(2)}) %collective-permute-start.3) | collective-permute-done | bytes 544 | tf_op jit(solution)/shard_map/ppermute | solution.py:16
  54.7 4.4 %collective-permute-start.5 = (bf16[256,1024]{0,1:T(8,128)(2,1)}, bf16[256,1024]{0,1:T(8,128)(2,1)S(1)}, u32[]{:S(2)}, u32[]{:S(2)}) collective-permute-start(bf16[256,1024]{0,1:T(8,128)(2,1)} %collective-permute-done.4), channel_id=1, source_target_pairs={{0,15},{1,0},{2,1},{3,2},{4,3},{5,4},{6,5},{7,6},{8,7},{9,8},{10,9... | collective-permute-start | bytes 1572872 | tf_op jit(solution)/shard_map/ppermute | solution.py:16
  59.2 1.3 pad_maximum_fusion.1
  61.6 7.3 %collective-permute-done.5 = bf16[256,1024]{0,1:T(8,128)(2,1)S(1)} collective-permute-done((bf16[256,1024]{0,1:T(8,128)(2,1)}, bf16[256,1024]{0,1:T(8,128)(2,1)S(1)}, u32[]{:S(2)}, u32[]{:S(2)}) %collective-permute-start.5) | collective-permute-done | bytes 524320 | tf_op jit(solution)/shard_map/ppermute | solution.py:16
  68.9 1.1 pad_maximum_fusion.2
  70.1 1.0 fusion.1
  74.2 13.0 %collective-permute-done.6 = bf16[256,1024]{0,1:T(8,128)(2,1)S(1)} collective-permute-done((bf16[256,1024]{0,1:T(8,128)(2,1)S(1)}, bf16[256,1024]{0,1:T(8,128)(2,1)S(1)}, u32[]{:S(2)}, u32[]{:S(2)}) %collective-permute-start.6) | collective-permute-done | bytes 524320 | tf_op jit(solution)/shard_map/ppermute | solution.py:16
  87.5 11.0 %collective-permute-done.8 = bf16[256,1024]{0,1:T(8,128)(2,1)S(1)} collective-permute-done((bf16[256,1024]{0,1:T(8,128)(2,1)S(1)}, bf16[256,1024]{0,1:T(8,128)(2,1)S(1)}, u32[]{:S(2)}, u32[]{:S(2)}) %collective-permute-start.8) | collective-permute-done | bytes 524320 | tf_op jit(solution)/shard_map/ppermute | solution.py:16
  98.9 10.8 %collective-permute-done.7 = bf16[256,1024]{0,1:T(8,128)(2,1)S(1)} collective-permute-done((bf16[256,1024]{0,1:T(8,128)(2,1)S(1)}, bf16[256,1024]{0,1:T(8,128)(2,1)S(1)}, u32[]{:S(2)}, u32[]{:S(2)}) %collective-permute-start.7) | collective-permute-done | bytes 524320 | tf_op jit(solution)/shard_map/ppermute | solution.py:16
  109.8 11.1 %collective-permute-done.9 = bf16[256,1024]{0,1:T(8,128)(2,1)S(1)} collective-permute-done((bf16[256,1024]{0,1:T(8,128)(2,1)S(1)}, bf16[256,1024]{0,1:T(8,128)(2,1)S(1)}, u32[]{:S(2)}, u32[]{:S(2)}) %collective-permute-start.9) | collective-permute-done | bytes 524320 | tf_op jit(solution)/shard_map/ppermute | solution.py:16
  121.1 6.4 %convert_bitcast_fusion = bf16[1024,3,2048]{2,0,1:T(8,128)(2,1)} fusion(bf16[256,1,1024]{0,2,1:T(8,128)(2,1)S(1)} %fusion.27, bf16[256,1,1024]{0,2,1:T(8,128)(2,1)S(1)} %fusion.26, bf16[256,1,1024]{0,2,1:T(8,128)(2,1)S(1)} %fusion.15, bf16[1,256,2048]{2,1,0:T(8,128)(2,1)S(1)} %copy-done), kind=kOutput, calls=%fused_computation.1 | convolution fusion | flops 3229089792 | bytes 15204352 | tf_op jit(solution)/shard_map/twh,td->hwd/dot_general | solution.py:151
  127.4 12.2 %pad_maximum_fusion = bf16[1024,4,2048]{2,0,1:T(8,128)(2,1)} fusion(bf16[1024,1,2048]{2,0,1:T(8,128)(2,1)S(1)} %copy-done.2, bf16[1024,3,2048]{2,0,1:T(8,128)(2,1)} %convert_bitcast_fusion), kind=kLoop, calls=%fused_computation | loop fusion | flops 8388608 | bytes 33554432 | tf_op jit(solution)/shard_map/concatenate | solution.py:158
  139.6 181.0 %reduce-scatter.2.cloned.1.call-done = bf16[64,4,2048]{2,0,1:T(8,128)(2,1)} async-done(((bf16[1024,4,2048]{2,0,1:T(8,128)(2,1)}), bf16[64,4,2048]{2,0,1:T(8,128)(2,1)}) %reduce-scatter.2.cloned.1.call-update) | async-done | bytes 1048592 | tf_op jit(solution)/shard_map/reduce_scatter | solution.py:157
  320.6 1.6 bitcast_bitcast_fusion
  322.3 34.3 %all_to_all.21 = bf16[16,64,4,128]{3,1,2,0:T(8,128)(2,1)S(1)} all-to-all(bf16[16,64,4,128]{3,1,2,0:T(8,128)(2,1)S(1)} %bitcast_bitcast_fusion), channel_id=1, replica_groups=mesh['dp'=16,'blk'=16] {'blk'}, dimensions={0} | all-to-all | bytes 2097152 | tf_op jit(solution)/shard_map/all_to_all | solution.py:30
  357.0 13.5 %all_to_all.22 = f32[16,1,256]{2,1,0:T(1,128)S(1)} all-to-all(f32[16,1,256]{2,1,0:T(1,128)S(1)} %reshape.171), channel_id=1, replica_groups=mesh['dp'=16,'blk'=16] {'blk'}, dimensions={0} | all-to-all | bytes 32768 | tf_op jit(solution)/shard_map/all_to_all | solution.py:36
  371.2 4.4 %all-to-all-start.1 = ((f32[16,4,128]{2,1,0:T(4,128)}), f32[16,4,128]{2,1,0:T(4,128)S(1)}, u32[]{:S(2)}, u32[]{:S(2)}) async-start(f32[16,4,128]{2,1,0:T(4,128)} %broadcast_in_dim.58), calls=%async_computation.2 | async-start | bytes 65536 | tf_op jit(solution)/shard_map/all_to_all | solution.py:36
  376.9 4.5 %all-to-all-done.1 = f32[16,4,128]{2,1,0:T(4,128)S(1)} async-done(((f32[16,4,128]{2,1,0:T(4,128)}), f32[16,4,128]{2,1,0:T(4,128)S(1)}, u32[]{:S(2)}, u32[]{:S(2)}) %all-to-all-start.1) | async-done | bytes 32800 | tf_op jit(solution)/shard_map/all_to_all | solution.py:36
  382.1 3.5 all-to-all-start.3
  385.7 8.7 %all-to-all-done.3 = f32[16,1,4]{2,1,0:T(1,128)S(1)} async-done(((f32[16,1,4]{2,1,0:T(1,128)}), f32[16,1,4]{2,1,0:T(1,128)S(1)}, u32[]{:S(2)}, u32[]{:S(2)}) %all-to-all-start.3) | async-done | bytes 288 | tf_op jit(solution)/shard_map/all_to_all | solution.py:36
  (93 shorter events, 12.2 us)
Async XLA Ops:
  7.2 113.9 %copy-start = (bf16[1,256,2048]{2,1,0:T(8,128)(2,1)S(1)}, bf16[1,256,2048]{2,1,0:T(8,128)(2,1)}, u32[]{:S(2)}) copy-start(bf16[1,256,2048]{2,1,0:T(8,128)(2,1)} %param.15) | copy-start | bytes 3145732
  7.2 15.5 %copy-start.10 = (bf16[1,256,1024]{2,1,0:T(8,128)(2,1)S(1)}, bf16[1,256,1024]{2,1,0:T(8,128)(2,1)}, u32[]{:S(2)}) copy-start(bf16[1,256,1024]{2,1,0:T(8,128)(2,1)} %param.20) | copy-start | bytes 1572868
  7.2 15.8 %copy-start.6 = (bf16[1,256,1024]{2,1,0:T(8,128)(2,1)S(1)}, bf16[1,256,1024]{2,1,0:T(8,128)(2,1)}, u32[]{:S(2)}) copy-start(bf16[1,256,1024]{2,1,0:T(8,128)(2,1)} %param.19) | copy-start | bytes 1572868
  7.2 313.4 %reduce-scatter.2.cloned.1.call-start = ((), (), s32[]{:S(2)}) async-start(), calls=%async_computation.5 | async-start | bytes 17825792 | tf_op jit(solution)/shard_map/reduce_scatter | solution.py:157
  8.1 29.5 %collective-permute-start.2 = (bf16[256]{0:T(256)(128)(2,1)S(1)}, bf16[256]{0:T(256)(128)(2,1)S(1)}, u32[]{:S(2)}, u32[]{:S(2)}) collective-permute-start(bf16[256]{0:T(256)(128)(2,1)S(1)} %convert_element_type.64), channel_id=1, source_target_pairs={{0,15},{1,0},{2,1},{3,2},{4,3},{5,4},{6,5},{7,6},{8,7},{9,8},{10,9... | collective-permute-start | bytes 1544 | tf_op jit(solution)/shard_map/ppermute | solution.py:16
  19.2 12.8 %collective-permute-start = (bf16[256,1024]{0,1:T(8,128)(2,1)}, bf16[256,1024]{0,1:T(8,128)(2,1)}, u32[]{:S(2)}, u32[]{:S(2)}) collective-permute-start(bf16[256,1024]{0,1:T(8,128)(2,1)} %bitcast.1), channel_id=1, source_target_pairs={{0,15},{1,0},{2,1},{3,2},{4,3},{5,4},{6,5},{7,6},{8,7},{9,8},{10,9... | collective-permute-start | bytes 1572872 | tf_op jit(solution)/shard_map/ppermute | solution.py:16
  21.9 32.8 %collective-permute-start.4 = (bf16[256,1024]{0,1:T(8,128)(2,1)}, bf16[256,1024]{0,1:T(8,128)(2,1)}, u32[]{:S(2)}, u32[]{:S(2)}) collective-permute-start(bf16[256,1024]{0,1:T(8,128)(2,1)} %bitcast.6), channel_id=1, source_target_pairs={{0,15},{1,0},{2,1},{3,2},{4,3},{5,4},{6,5},{7,6},{8,7},{9,8},{10,9... | collective-permute-start | bytes 1572872 | tf_op jit(solution)/shard_map/ppermute | solution.py:16
  23.9 13.6 %copy-start.11 = (bf16[1,256,1024]{2,1,0:T(8,128)(2,1)S(1)}, bf16[1,256,1024]{2,1,0:T(8,128)(2,1)}, u32[]{:S(2)}) copy-start(bf16[1,256,1024]{2,1,0:T(8,128)(2,1)} %param.16) | copy-start | bytes 1572868
  32.0 27.1 %collective-permute-start.1 = (bf16[256,1024]{0,1:T(8,128)(2,1)}, bf16[256,1024]{0,1:T(8,128)(2,1)}, u32[]{:S(2)}, u32[]{:S(2)}) collective-permute-start(bf16[256,1024]{0,1:T(8,128)(2,1)} %collective-permute-done), channel_id=1, source_target_pairs={{0,15},{1,0},{2,1},{3,2},{4,3},{5,4},{6,5},{7,6},{8,7},{9,8},{10,9... | collective-permute-start | bytes 1572872 | tf_op jit(solution)/shard_map/ppermute | solution.py:16
  37.5 2.7 copy-start.9
  37.5 17.0 %collective-permute-start.3 = (bf16[256]{0:T(256)(128)(2,1)S(1)}, bf16[256]{0:T(256)(128)(2,1)S(1)}, u32[]{:S(2)}, u32[]{:S(2)}) collective-permute-start(bf16[256]{0:T(256)(128)(2,1)S(1)} %collective-permute-done.2), channel_id=1, source_target_pairs={{0,15},{1,0},{2,1},{3,2},{4,3},{5,4},{6,5},{7,6},{8,7},{9,8},{10,9... | collective-permute-start | bytes 1544 | tf_op jit(solution)/shard_map/ppermute | solution.py:16
  40.2 14.3 %copy-start.18 = (s32[1,256]{1,0:T(1,128)S(1)}, s32[1,256]{1,0:T(1,128)}, u32[]{:S(2)}) copy-start(s32[1,256]{1,0:T(1,128)} %param.26) | copy-start | bytes 3076
  43.2 17.3 %copy-start.7 = (bf16[1,256,1024]{1,2,0:T(8,128)(2,1)S(1)}, bf16[1,256,1024]{1,2,0:T(8,128)(2,1)}, u32[]{:S(2)}) copy-start(bf16[1,256,1024]{1,2,0:T(8,128)(2,1)} %copy.104) | copy-start | bytes 1572868
  54.7 14.2 %collective-permute-start.5 = (bf16[256,1024]{0,1:T(8,128)(2,1)}, bf16[256,1024]{0,1:T(8,128)(2,1)S(1)}, u32[]{:S(2)}, u32[]{:S(2)}) collective-permute-start(bf16[256,1024]{0,1:T(8,128)(2,1)} %collective-permute-done.4), channel_id=1, source_target_pairs={{0,15},{1,0},{2,1},{3,2},{4,3},{5,4},{6,5},{7,6},{8,7},{9,8},{10,9... | collective-permute-start | bytes 1572872 | tf_op jit(solution)/shard_map/ppermute | solution.py:16
  61.1 8.9 %copy-start.8 = (bf16[256,4,256]{0,2,1:T(8,128)(2,1)S(1)}, bf16[256,4,256]{0,2,1:T(8,128)(2,1)}, u32[]{:S(2)}) copy-start(bf16[256,4,256]{0,2,1:T(8,128)(2,1)} %copy.91) | copy-start | bytes 1572868
  71.5 1.4 copy-start.4
  71.6 15.6 %collective-permute-start.6 = (bf16[256,1024]{0,1:T(8,128)(2,1)S(1)}, bf16[256,1024]{0,1:T(8,128)(2,1)S(1)}, u32[]{:S(2)}, u32[]{:S(2)}) collective-permute-start(bf16[256,1024]{0,1:T(8,128)(2,1)S(1)} %bitcast.125), channel_id=1, source_target_pairs={{0,1},{1,2},{2,3},{3,4},{4,5},{5,6},{6,7},{7,8},{8,9},{9,10},{10,1... | collective-permute-start | bytes 1572872 | tf_op jit(solution)/shard_map/ppermute | solution.py:16
  73.0 14.3 %slice-start.1 = ((f32[512,4,256]{0,2,1:T(8,128)}), f32[256,4,256]{0,2,1:T(8,128)S(1)}, s32[]{:S(2)}) async-start(f32[512,4,256]{0,2,1:T(8,128)} %copy-done.4), calls=%async_computation.7 | async-start | bytes 2097152 | tf_op jit(solution)/shard_map/slice | solution.py:135
  73.0 25.5 %collective-permute-start.8 = (bf16[256,1024]{0,1:T(8,128)(2,1)S(1)}, bf16[256,1024]{0,1:T(8,128)(2,1)S(1)}, u32[]{:S(2)}, u32[]{:S(2)}) collective-permute-start(bf16[256,1024]{0,1:T(8,128)(2,1)S(1)} %bitcast.126), channel_id=1, source_target_pairs={{0,1},{1,2},{2,3},{3,4},{4,5},{5,6},{6,7},{7,8},{8,9},{9,10},{10,1... | collective-permute-start | bytes 1572872 | tf_op jit(solution)/shard_map/ppermute | solution.py:16
  74.2 24.5 %copy-start.5 = (f32[1,256,1024]{1,2,0:T(8,128)S(1)}, f32[1,256,1024]{1,2,0:T(8,128)}, u32[]{:S(2)}) copy-start(f32[1,256,1024]{1,2,0:T(8,128)} %copy.77) | copy-start | bytes 3145732
  87.2 11.2 %slice-start = ((f32[512,4,256]{0,2,1:T(8,128)}), f32[256,4,256]{0,2,1:T(8,128)S(1)}, s32[]{:S(2)}) async-start(f32[512,4,256]{0,2,1:T(8,128)} %copy-done.3), calls=%async_computation.6 | async-start | bytes 2097152 | tf_op jit(solution)/shard_map/slice | solution.py:135
  87.4 22.3 %collective-permute-start.7 = (bf16[256,1024]{0,1:T(8,128)(2,1)S(1)}, bf16[256,1024]{0,1:T(8,128)(2,1)S(1)}, u32[]{:S(2)}, u32[]{:S(2)}) collective-permute-start(bf16[256,1024]{0,1:T(8,128)(2,1)S(1)} %fusion.20), channel_id=1, source_target_pairs={{0,1},{1,2},{2,3},{3,4},{4,5},{5,6},{6,7},{7,8},{8,9},{9,10},{10,1... | collective-permute-start | bytes 1572872 | tf_op jit(solution)/shard_map/ppermute | solution.py:16
  98.6 22.3 %collective-permute-start.9 = (bf16[256,1024]{0,1:T(8,128)(2,1)S(1)}, bf16[256,1024]{0,1:T(8,128)(2,1)S(1)}, u32[]{:S(2)}, u32[]{:S(2)}) collective-permute-start(bf16[256,1024]{0,1:T(8,128)(2,1)S(1)} %fusion.18), channel_id=1, source_target_pairs={{0,1},{1,2},{2,3},{3,4},{4,5},{5,6},{6,7},{7,8},{8,9},{9,10},{10,1... | collective-permute-start | bytes 1572872 | tf_op jit(solution)/shard_map/ppermute | solution.py:16
  121.1 6.4 %copy-start.2 = (bf16[1024,1,2048]{2,0,1:T(8,128)(2,1)S(1)}, bf16[1024,1,2048]{2,0,1:T(8,128)(2,1)}, u32[]{:S(2)}) copy-start(bf16[1024,1,2048]{2,0,1:T(8,128)(2,1)} %convert_bitcast_fusion.1) | copy-start | bytes 12582916
  320.6 74.5 %copy-start.1 = (bf16[1,256,2048]{2,1,0:T(8,128)(2,1)S(1)}, bf16[1,256,2048]{2,1,0:T(8,128)(2,1)}, u32[]{:S(2)}) copy-start(bf16[1,256,2048]{2,1,0:T(8,128)(2,1)} %param.15) | copy-start | bytes 3145732
  322.2 59.2 %copy-start.17 = (f32[4,128]{1,0:T(4,128)S(1)}, f32[4,128]{1,0:T(4,128)}, u32[]{:S(2)}) copy-start(f32[4,128]{1,0:T(4,128)} %param.28) | copy-start | bytes 6148
  322.3 63.4 %copy-start.16 = (f32[4,64]{1,0:T(4,128)S(1)}, f32[4,64]{1,0:T(4,128)}, u32[]{:S(2)}) copy-start(f32[4,64]{1,0:T(4,128)} %param.29) | copy-start | bytes 3076
  322.3 72.1 %copy-start.12 = (f32[4,128,64]{1,2,0:T(8,128)S(1)}, f32[4,128,64]{1,2,0:T(8,128)}, u32[]{:S(2)}) copy-start(f32[4,128,64]{1,2,0:T(8,128)} %param.27) | copy-start | bytes 393220
  371.2 10.2 %all-to-all-start.1 = ((f32[16,4,128]{2,1,0:T(4,128)}), f32[16,4,128]{2,1,0:T(4,128)S(1)}, u32[]{:S(2)}, u32[]{:S(2)}) async-start(f32[16,4,128]{2,1,0:T(4,128)} %broadcast_in_dim.58), calls=%async_computation.2 | async-start | bytes 65536 | tf_op jit(solution)/shard_map/all_to_all | solution.py:36
  381.5 13.6 %copy-start.15 = (f32[4,128]{1,0:T(4,128)}, f32[4,128]{1,0:T(4,128)S(1)}, u32[]{:S(2)}) copy-start(f32[4,128]{1,0:T(4,128)S(1)} %get-tuple-element.6) | copy-start | bytes 6148
  382.1 12.2 %all-to-all-start.3 = ((f32[16,1,4]{2,1,0:T(1,128)}), f32[16,1,4]{2,1,0:T(1,128)S(1)}, u32[]{:S(2)}, u32[]{:S(2)}) async-start(f32[16,1,4]{2,1,0:T(1,128)} %broadcast_in_dim.60), calls=%async_computation.4 | async-start | bytes 16384 | tf_op jit(solution)/shard_map/all_to_all | solution.py:36
  385.6 9.5 %copy-start.14 = (f32[4,64]{1,0:T(4,128)}, f32[4,64]{1,0:T(4,128)S(1)}, u32[]{:S(2)}) copy-start(f32[4,64]{1,0:T(4,128)S(1)} %multiply_add_fusion.1) | copy-start | bytes 3076
  (2 other events, 2.0 us)
Sparse Core Ops, SparseCore 0:
  139.8 180.8 reduce-scatter.1
where the time goes:
time: 403 us; the launch traced here: 402 us
  waiting for transfers between devices  262 us (65%)
  blocking collectives  47.8 us (12%)
  starting transfers between devices  27.7 us (7%)
  other arithmetic  19.2 us (5%)
  local copies, waits for them, and re-layouts  16.6 us (4%)
  between operations  14.4 us (4%)
  matrix products  14 us (3%)
    reduce_scatter x1, waiting for transfers between devices, body(): lax.psum_scatter(jnp.concatenate([part_inner, part_output[:, None, :]], a...  181 us
    ppermute x10, waiting for transfers between devices, passed_along(): return lax.ppermute(value, axis, pairs)  68.1 us
    all_to_all x1, blocking collectives, sum_at_owner(): lax.all_to_all(in_blocks(array, dim, devices), axis, 0, 0, tiled=True)  34.3 us
    ppermute x10, starting transfers between devices, passed_along(): return lax.ppermute(value, axis, pairs)  19.8 us
    all_to_all x1, blocking collectives, from_everyone(): lax.all_to_all(jnp.broadcast_to(array[None], (devices, *array.shape)), ax...  13.5 us
    all_to_all x2, waiting for transfers between devices, from_everyone(): lax.all_to_all(jnp.broadcast_to(array[None], (devices, *array.shape)), ax...  13.2 us
    concatenate x1, other arithmetic, body(): jnp.concatenate([part_inner, part_output[:, None, :]], axis=1)  12.2 us
    unnamed x45, local copies, waits for them, and re-layouts  9.99 us
  transfers between devices with their start and end apart: 13, of which 10 were waited for; matrix products, arithmetic and copies ran while one was open for 6% of the time, Pallas kernels for 0%

commit v1 on v0

v1 whole, which is shorter than its diff:
```python
from types import SimpleNamespace

import jax
import jax.numpy as jnp
from jax import lax
from jax.experimental import pallas as pl
from jax.experimental.pallas import tpu as pltpu
from jax.sharding import PartitionSpec as P

beta_two = 0.9
learn_rate = 0.05
tiny_square = 1e-30
low = jnp.bfloat16
full = jnp.float32
ALL_TOKENS = 65536.0
SCALE = 1.0 / 16.0

NT = (((1,), (1,)), ((), ()))
NN = (((1,), (0,)), ((), ()))
TN = (((0,), (0,)), ((), ()))


def dot(a, b, dims):
    return lax.dot_general(a, b, dims, preferred_element_type=full)


def group_scratch(tag, w):
    return {
        "p_" + tag: pltpu.VMEM((4, 2, 4, w, 64, 512), low),
        "xa_" + tag: pltpu.VMEM((2, 2, w, 64, 512), low),
        "xb_" + tag: pltpu.VMEM((2, 4, w, 64, 512), low),
        "ya_" + tag: pltpu.VMEM((2, w, 32, 512), low),
        "yb_" + tag: pltpu.VMEM((2, w, 64, 512), low),
        "ea_" + tag: pltpu.VMEM((4, 2, w, 32, 512), low),
        "eb_" + tag: pltpu.VMEM((4, 2, w, 64, 512), low),
        "fa_" + tag: pltpu.VMEM((2, w, 32, 512), low),
        "fb_" + tag: pltpu.VMEM((2, w, 64, 512), low),
        "zs_" + tag: pltpu.VMEM((8, w, 64, 128), low),
        "zr_" + tag: pltpu.VMEM((8, w, 64, 128), low),
        "rtf_" + tag: pltpu.VMEM((4, w, 2, 2, 64, 256), low),
        "rtp_" + tag: pltpu.VMEM((4, w, 2, 64, 256), low),
    }


N_SEM = 160
SCRATCH = {
    "ly": pltpu.VMEM((2, 256, 2048), low),
    "gt": pltpu.VMEM((2, 256, 2048), low),
    "cx": pltpu.VMEM((4, 256, 256), low),
    "gox": pltpu.VMEM((4, 256, 256), low),
    "kk": pltpu.VMEM((4, 512, 256), low),
    "vv": pltpu.VMEM((4, 512, 256), low),
    "qr": pltpu.VMEM((4, 2, 128, 256), low),
    "orr": pltpu.VMEM((4, 2, 128, 256), low),
    "gqs": pltpu.VMEM((4, 256, 256), full),
    "gks": pltpu.VMEM((4, 256, 256), full),
    "gvs": pltpu.VMEM((4, 256, 256), full),
    "meta": pltpu.VMEM((4, 8, 256), full),
    "mr": pltpu.VMEM((4, 8, 256), full),
    "ds": pltpu.VMEM((8, 256), full),
    "dr": pltpu.VMEM((8, 256), full),
    "dk": pltpu.VMEM((512, 128), full),
    "acck": pltpu.VMEM((256, 256), full),
    "accv": pltpu.VMEM((256, 256), full),
    "dqs": pltpu.VMEM((4, 2, 128, 256), low),
    "dks": pltpu.VMEM((4, 256, 256), low),
    "dvs": pltpu.VMEM((4, 256, 256), low),
    "dqr": pltpu.VMEM((4, 2, 128, 256), low),
    "dkr": pltpu.VMEM((4, 256, 256), low),
    "dvr": pltpu.VMEM((4, 256, 256), low),
    "rows": pltpu.VMEM((8, 128), full),
    "cols": pltpu.VMEM((8, 128), full),
    "tot": pltpu.VMEM((8, 128), full),
    "rowr": pltpu.VMEM((16, 8, 128), full),
    "colr": pltpu.VMEM((16, 8, 128), full),
    "totr": pltpu.VMEM((16, 8, 128), full),
    "grad": pltpu.VMEM((4, 64, 128), full),
    **group_scratch("o", 1),
    **group_scratch("m", 3),
    "send": pltpu.SemaphoreType.DMA((N_SEM,)),
    "recv": pltpu.SemaphoreType.DMA((N_SEM,)),
    "local": pltpu.SemaphoreType.DMA((40,)),
    "stat_send": pltpu.SemaphoreType.DMA((3, 16)),
    "stat_recv": pltpu.SemaphoreType.DMA((3, 16)),
}


def kernel(lay, q, k, v, ctx, go, gout, mass, gq, gk, gv, docs, wts, rf, cf, ow, orf, ocf, *scr):
    s = SimpleNamespace(**dict(zip(SCRATCH, scr)))
    dp = lax.axis_index("dp")
    b = lax.axis_index("blk")
    x = lax.div(dp, 4)
    yl = lax.rem(lax.div(dp, 2), 2)
    c = lax.rem(dp, 2)
    yh = lax.div(b, 8)
    z = lax.rem(b, 8)
    y = yh * 2 + yl

    def at(x_, y_, z_):
        return {"dp": x_ * 4 + lax.rem(y_, 2) * 2 + c, "blk": lax.div(y_, 2) * 8 + z_}

    up_x, dn_x = at(lax.rem(x + 1, 4), y, z), at(lax.rem(x + 3, 4), y, z)
    up_y, dn_y = at(x, lax.rem(y + 1, 4), z), at(x, lax.rem(y + 3, 4), z)
    y_one, y_two, y_three = lax.rem(y + 1, 4), lax.rem(y + 2, 4), lax.rem(y + 3, 4)
    mate = {"dp": dp + 1 - 2 * c, "blk": b}
    up_b, dn_b = {"dp": dp, "blk": lax.rem(b + 1, 16)}, {"dp": dp, "blk": lax.rem(b + 15, 16)}
    heads = [lax.rem(x + 2, 4), lax.rem(x + 1, 4), lax.rem(x + 3, 4), x]
    cols = [pl.ds(pl.multiple_of(h * 256, 256), 256) for h in heads]

    barrier = pltpu.get_barrier_semaphore()

    def greet(p, carry):
        pl.semaphore_signal(
            barrier, inc=1, device_id={"dp": lax.rem(dp + p, 16), "blk": b},
            device_id_type=pl.DeviceIdType.MESH,
        )
        pl.semaphore_signal(
            barrier, inc=1, device_id={"dp": dp, "blk": lax.rem(b + p, 16)},
            device_id_type=pl.DeviceIdType.MESH,
        )
        return carry

    lax.fori_loop(1, 16, greet, 0)
    pl.semaphore_signal(
        barrier, inc=1, device_id=at(x, 3 - y, z), device_id_type=pl.DeviceIdType.MESH
    )

    used = [0, 0]
    to_finish = []

    def local(src, dst):
        copy = pltpu.make_async_copy(src, dst, s.local.at[used[1]])
        used[1] += 1
        copy.start()
        return copy

    def remote(src, dst, device, cond=None):
        n = used[0]
        used[0] += 1
        copy = pltpu.make_async_remote_copy(
            src_ref=src, dst_ref=dst, send_sem=s.send.at[n], recv_sem=s.recv.at[n],
            device_id=device, device_id_type=pl.DeviceIdType.MESH,
        )
        if cond is None:
            copy.start()
        else:
            @pl.when(cond)
            def _():
                copy.start()
        to_finish.append((copy, cond))
        return copy

    def arrived(copy, cond=None):
        if cond is None:
            copy.wait_recv()
        else:
            @pl.when(cond)
            def _():
                copy.wait_recv()

    wrapped = (b == 0) | (b == 15)
    sends_low_q = b >= 14
    sends_up_k = b >= 2
    plain = (b >= 1) & (b <= 14)

    load_cx = [local(ctx.at[:, cols[i]], s.cx.at[i]) for i in range(4)]
    load_go = [local(go.at[:, cols[i]], s.gox.at[i]) for i in range(4)]
    load_kv = []
    for i in range(4):
        load_kv.append(
            (
                local(k.at[:, cols[i]], s.kk.at[i, pl.ds(0, 256)]),
                local(v.at[:, cols[i]], s.vv.at[i, pl.ds(0, 256)]),
            )
        )
    load_gt = local(gout, s.gt.at[0])
    load_ly = local(lay, s.ly.at[0])
    load_g = []
    for i in range(4):
        load_g.append(
            (
                local(gq.at[:, cols[i]], s.gqs.at[i]),
                local(gk.at[:, cols[i]], s.gks.at[i]),
                local(gv.at[:, cols[i]], s.gvs.at[i]),
            )
        )

    own_docs = docs[...].astype(full)
    s.ds[...] = jnp.broadcast_to(own_docs, (8, 256))
    s.dk[pl.ds(0, 256), :] = jnp.transpose(jnp.broadcast_to(own_docs, (128, 256)))
    ones = jnp.ones((8, 256), low)
    for i in range(4):
        load_cx[i].wait()
        load_go[i].wait()
        product = s.cx[i].astype(full) * s.gox[i].astype(full)
        high_part = product.astype(low)
        low_part = (product - high_part.astype(full)).astype(low)
        row_dot = dot(ones, high_part, NT) + dot(ones, low_part, NT)
        s.meta[i, pl.ds(0, 1), :] = mass[pl.ds(heads[i], 1), :]
        s.meta[i, pl.ds(1, 1), :] = row_dot[0:1, :]
        s.meta[i, pl.ds(2, 1), :] = own_docs
        s.rtf_o[i, 0] = jnp.transpose(s.cx[i]).reshape(2, 2, 64, 256)

    @pl.when(wrapped)
    def _():
        for i in range(4):
            s.kk[i, pl.ds(384, 128), :] = jnp.zeros((128, 256), low)
            s.vv[i, pl.ds(384, 128), :] = jnp.zeros((128, 256), low)

    pl.semaphore_wait(barrier, 31)

    lower, upper = pl.ds(0, 128), pl.ds(128, 128)
    go_meta = remote(s.meta, s.mr, up_b)
    go_docs = remote(s.ds, s.dr, dn_b)
    send_rto = remote(s.rtf_o.at[:, :, :, 1 - c], s.rtp_o, mate)
    send_gt = remote(gout, s.gt.at[1], mate)
    forward = []
    for i in range(4):
        forward.append(
            [
                (remote(k.at[lower, cols[i]], s.kk.at[i, pl.ds(256, 128)], dn_b), None),
                (remote(q.at[upper, cols[i]], s.qr.at[i, 0], up_b), None),
                (remote(k.at[upper, cols[i]], s.kk.at[i, pl.ds(384, 128)], dn_b, sends_up_k), plain),
                (remote(q.at[lower, cols[i]], s.qr.at[i, 1], up_b, sends_low_q), wrapped),
                (remote(v.at[lower, cols[i]], s.vv.at[i, pl.ds(256, 128)], dn_b), None),
                (remote(go.at[upper, cols[i]], s.orr.at[i, 0], up_b), None),
                (remote(v.at[upper, cols[i]], s.vv.at[i, pl.ds(384, 128)], dn_b, sends_up_k), plain),
                (remote(go.at[lower, cols[i]], s.orr.at[i, 1], up_b, sends_low_q), wrapped),
            ]
        )
    send_ly = remote(lay, s.ly.at[1], mate)

    def weight_part(left, mate_left, right, p_ref, i, w):
        def block(db, carry):
            lanes = pl.ds(pl.multiple_of(db * 256, 256), 256)
            out = dot(left, right[0, :, lanes], NN) + dot(mate_left, right[1, :, lanes], NN)
            out = out.astype(low).reshape(-1, w, 2, 64, 256)
            y_hi = lax.div(db, 4)
            half = lax.rem(lax.div(db, 2), 2)
            at_lane = pl.ds(pl.multiple_of(lax.rem(db, 2) * 256, 256), 256)
            for n in range(out.shape[0]):
                for one in range(2):
                    p_ref[i + n, half, y_hi * 2 + one, :, :, at_lane] = out[n, :, one]
            return carry

        lax.fori_loop(0, 8, block, 0)

    def add_to(ref, *others):
        total = ref[...].astype(full)
        for other in others:
            total = total + other[...].astype(full)
        ref[...] = total.astype(low)

    top, bottom = pl.ds(0, 32), pl.ds(32, 32)

    class Group:
        def __init__(self, tag, w):
            self.w = w
            for name in ("p", "xa", "xb", "ya", "yb", "ea", "eb", "fa", "fb", "zs", "zr", "rtf", "rtp"):
                setattr(self, name, getattr(s, name + "_" + tag))
            self.ea_copy, self.eb_copy = {}, {}

        def x_first(self, i):
            p = self.p
            if i == 0:
                self.xa0 = remote(p.at[0, 0, pl.ds(0, 2)], self.xa.at[0], up_x)
                self.xa1 = remote(p.at[0, 0, pl.ds(2, 2)], self.xa.at[1], dn_x)
            elif i == 1:
                arrived(self.xa0)
                add_to(p.at[1, 0, pl.ds(0, 2)], self.xa.at[0])
                self.xb0 = remote(p.at[1, 0], self.xb.at[0], up_x)
            elif i == 2:
                arrived(self.xa1)
                add_to(p.at[2, 0, pl.ds(2, 2)], self.xa.at[1])
                self.xb1 = remote(p.at[2, 0], self.xb.at[1], dn_x)

        def x_first_end(self):
            p = self.p
            arrived(self.xb0)
            arrived(self.xb1)
            add_to(p.at[3, 0], self.xb.at[0], self.xb.at[1])
            self.ya0 = remote(p.at[3, 0, y_two, :, top], self.ya.at[0], up_y)
            self.ya1 = remote(p.at[3, 0, y_two, :, bottom], self.ya.at[1], dn_y)

        def then_y(self):
            p = self.p
            arrived(self.ya0)
            add_to(p.at[3, 0, y_one, :, top], self.ya.at[0])
            self.yb0 = remote(p.at[3, 0, y_one], self.yb.at[0], up_y)
            arrived(self.ya1)
            add_to(p.at[3, 0, y_three, :, bottom], self.ya.at[1])
            self.yb1 = remote(p.at[3, 0, y_three], self.yb.at[1], dn_y)

        def y_first(self, i):
            p = self.p
            self.ea_copy[i] = (
                remote(p.at[i, 1, y_two, :, top], self.ea.at[i, 0], up_y),
                remote(p.at[i, 1, y_two, :, bottom], self.ea.at[i, 1], dn_y),
            )

        def y_second(self, i):
            p = self.p
            arrived(self.ea_copy[i][0])
            add_to(p.at[i, 1, y_one, :, top], self.ea.at[i, 0])
            first = remote(p.at[i, 1, y_one], self.eb.at[i, 0], up_y)
            arrived(self.ea_copy[i][1])
            add_to(p.at[i, 1, y_three, :, bottom], self.ea.at[i, 1])
            self.eb_copy[i] = (first, remote(p.at[i, 1, y_three], self.eb.at[i, 1], dn_y))

        def y_end_then_x(self, i):
            p = self.p
            arrived(self.eb_copy[i][0])
            arrived(self.eb_copy[i][1])
            mine = p.at[i, 1, y]
            add_to(mine, self.eb.at[i, 0], self.eb.at[i, 1])
            if i == 0:
                self.fa0 = remote(p.at[0, 1, y, :, top], self.fa.at[0], up_x)
                self.fa1 = remote(p.at[0, 1, y, :, bottom], self.fa.at[1], dn_x)
            elif i == 1:
                arrived(self.fa0)
                add_to(p.at[1, 1, y, :, top], self.fa.at[0])
                self.fb0 = remote(mine, self.fb.at[0], up_x)
            elif i == 2:
                arrived(self.fa1)
                add_to(p.at[2, 1, y, :, bottom], self.fa.at[1])
                self.fb1 = remote(mine, self.fb.at[1], dn_x)

        def stage(self, mine, one, two, base):
            total = mine[...].astype(full) + one[...].astype(full) + two[...].astype(full)
            total = total.astype(low)
            for n in range(4):
                self.zs[base + n] = total[:, :, n * 128 : (n + 1) * 128]

        def along_z(self):
            arrived(self.yb0)
            arrived(self.yb1)
            self.stage(self.p.at[3, 0, y], self.yb.at[0], self.yb.at[1], 0)
            arrived(self.fb0)
            arrived(self.fb1)
            self.stage(self.p.at[3, 1, y], self.fb.at[0], self.fb.at[1], 4)
            self.z_copies = []
            for p in (4, 3, 5, 2, 6, 1, 7):
                there = lax.rem(z + p, 8)
                self.z_copies.append(remote(self.zs.at[there], self.zr.at[p], at(x, y, there)))

        def total(self):
            for copy in self.z_copies:
                arrived(copy)
            total = self.zs[z].astype(full)
            for p in range(1, 8):
                total = total + self.zr[p].astype(full)
            return total

    out_g, main_g = Group("o", 1), Group("m", 3)

    load_gt.wait()
    arrived(send_rto)
    arrived(send_gt)
    weight_part(
        s.rtf_o[:, :, :, c].reshape(512, 256), s.rtp_o[...].reshape(512, 256), s.gt, s.p_o, 0, 1
    )
    out_g.x_first(0)
    for i in range(4):
        out_g.y_first(i)

    j = lax.rem(b + 15, 16)
    halves_here = jnp.where(wrapped, 2, 1)
    row = lax.broadcasted_iota(jnp.int32, (512, 128), 0)
    key_block = jnp.where(row < 256, b, lax.rem(b + 1, 16))
    key_low = (row < 128) | ((row >= 256) & (row < 384))
    key_place = jnp.where(key_low, key_block, 31 - key_block)

    returns = {}

    def attention(i):
        for copy, cond in forward[i]:
            arrived(copy, cond)
        for copy in load_kv[i] + load_g[i]:
            copy.wait()
        s.acck[...] = jnp.zeros((256, 256), full)
        s.accv[...] = jnp.zeros((256, 256), full)

        def one_half(r, carry):
            lanes = pl.ds(pl.multiple_of((1 - r) * 128, 128), 128)
            query = s.qr[i, r]
            grad = s.orr[i, r]
            mass_row = s.mr[i, pl.ds(0, 1), lanes]
            dot_row = s.mr[i, pl.ds(1, 1), lanes]
            docs_row = s.mr[i, pl.ds(2, 1), lanes]
            place = jnp.where(r == 0, 31 - j, j)
            open_pairs = (s.dk[...] == docs_row) & (key_place < place)
            keys = s.kk[i]
            scores = dot(keys, query, NT) * SCALE
            scores = jnp.where(open_pairs, scores, -jnp.inf)
            peak = jnp.maximum(mass_row, jnp.max(scores, axis=0, keepdims=True))
            shifted = jnp.exp(scores - peak)
            norm = jnp.exp(mass_row - peak) + jnp.sum(shifted, axis=0, keepdims=True)
            attention_part = shifted * (1.0 / norm)
            grad_attention = dot(s.vv[i], grad, NT)
            grad_scores = (attention_part * (grad_attention - dot_row) * SCALE).astype(low)
            value_step = dot(attention_part.astype(low), grad, NN)
            key_step = dot(grad_scores, query, NN)
            s.gks[i] += key_step[0:256]
            s.gvs[i] += value_step[0:256]
            s.acck[...] += key_step[256:512]
            s.accv[...] += value_step[256:512]
            s.dqs[i, r] = dot(jnp.transpose(grad_scores), keys, NN).astype(low)
            return carry

        lax.fori_loop(0, halves_here, one_half, 0)
        s.dks[i] = s.acck[...].astype(low)
        s.dvs[i] = s.accv[...].astype(low)
        returns[i] = [
            (remote(s.dqs.at[i, 0], s.dqr.at[i, 0], dn_b), None),
            (remote(s.dqs.at[i, 1], s.dqr.at[i, 1], dn_b, wrapped), sends_low_q),
            (remote(s.dks.at[i, lower], s.dkr.at[i, lower], up_b), None),
            (remote(s.dks.at[i, upper], s.dkr.at[i, upper], up_b, plain), sends_up_k),
            (remote(s.dvs.at[i, lower], s.dvr.at[i, lower], up_b), None),
            (remote(s.dvs.at[i, upper], s.dvr.at[i, upper], up_b, plain), sends_up_k),
        ]

    exchanged = {}

    def finalize(i):
        for copy, cond in returns[i]:
            arrived(copy, cond)
        s.gqs[i, upper, :] += s.dqr[i, 0].astype(full)
        s.gks[i, lower, :] += s.dkr[i, lower, :].astype(full)
        s.gvs[i, lower, :] += s.dvr[i, lower, :].astype(full)

        @pl.when(sends_low_q)
        def _():
            s.gqs[i, lower, :] += s.dqr[i, 1].astype(full)

        @pl.when(sends_up_k)
        def _():
            s.gks[i, upper, :] += s.dkr[i, upper, :].astype(full)
            s.gvs[i, upper, :] += s.dvr[i, upper, :].astype(full)

        for w, total in enumerate((s.gqs, s.gks, s.gvs)):
            s.rtf_m[i, w] = jnp.transpose(total[i].astype(low)).reshape(2, 2, 64, 256)
        exchanged[i] = remote(s.rtf_m.at[i, :, :, 1 - c], s.rtp_m.at[i], mate)

    def weights_of(i):
        arrived(exchanged[i])
        weight_part(
            s.rtf_m[i, :, :, c].reshape(384, 256), s.rtp_m[i].reshape(384, 256), s.ly, s.p_m, i, 3
        )
        main_g.x_first(i)
        main_g.y_first(i)

    arrived(go_meta)
    arrived(go_docs)
    s.dk[pl.ds(256, 256), :] = jnp.transpose(jnp.broadcast_to(s.dr[0:1, :], (128, 256)))
    attention(0)
    out_g.x_first(1)
    out_g.x_first(2)
    for i in range(4):
        out_g.y_second(i)
    attention(1)
    finalize(0)
    for i in range(3):
        out_g.y_end_then_x(i)
    out_g.x_first_end()
    load_ly.wait()
    arrived(send_ly)
    weights_of(0)
    attention(2)
    finalize(1)
    main_g.y_second(0)
    weights_of(1)
    out_g.y_end_then_x(3)
    out_g.then_y()
    attention(3)
    finalize(2)
    main_g.y_end_then_x(0)
    main_g.y_second(1)
    weights_of(2)
    out_g.along_z()
    finalize(3)
    main_g.y_end_then_x(1)
    main_g.y_second(2)
    weights_of(3)
    main_g.y_end_then_x(2)
    main_g.x_first_end()
    main_g.y_second(3)
    main_g.then_y()
    main_g.y_end_then_x(3)
    main_g.along_z()
    s.grad[3] = out_g.total()[0] * (1.0 / ALL_TOKENS)
    s.grad[pl.ds(0, 3)] = main_g.total() * (1.0 / ALL_TOKENS)

    s.rows[...] = jnp.zeros((8, 128), full)
    s.cols[...] = jnp.zeros((8, 128), full)
    for w in range(4):
        squares = s.grad[w] * s.grad[w] + tiny_square
        s.rows[pl.ds(w, 1), :] = jnp.sum(squares, axis=0, keepdims=True)
        s.cols[pl.ds(w, 1), pl.ds(0, 64)] = jnp.sum(jnp.transpose(squares), axis=0, keepdims=True)
    s.rowr[pl.ds(0, 1)] = s.rows[...][None]
    s.colr[pl.ds(0, 1)] = s.cols[...][None]

    def stat_copy(src, dst, n, p, device):
        return pltpu.make_async_remote_copy(
            src_ref=src, dst_ref=dst, send_sem=s.stat_send.at[n, p], recv_sem=s.stat_recv.at[n, p],
            device_id=device, device_id_type=pl.DeviceIdType.MESH,
        )

    def row_copy(p):
        return stat_copy(s.rows, s.rowr.at[p], 0, p, {"dp": lax.rem(dp + p, 16), "blk": b})

    def col_copy(p):
        return stat_copy(s.cols, s.colr.at[p], 1, p, {"dp": dp, "blk": lax.rem(b + p, 16)})

    def tot_copy(p):
        return stat_copy(s.tot, s.totr.at[p], 2, p, {"dp": dp, "blk": lax.rem(b + p, 16)})

    def each(action):
        def step(p, carry):
            action(p)
            return carry

        lax.fori_loop(1, 16, step, 0)

    each(lambda p: row_copy(p).start())
    each(lambda p: col_copy(p).start())
    each(lambda p: row_copy(p).wait_recv())
    row_sum = jnp.sum(s.rowr[...], axis=0)[0:4]
    new_row = beta_two * rf[...] + (1.0 - beta_two) * (row_sum / 1024.0)
    orf[...] = new_row
    s.tot[...] = jnp.zeros((8, 128), full)
    s.tot[pl.ds(0, 4), :] = new_row
    s.totr[pl.ds(0, 1)] = s.tot[...][None]
    each(lambda p: tot_copy(p).start())
    each(lambda p: col_copy(p).wait_recv())
    col_sum = jnp.sum(s.colr[...], axis=0)[0:4, 0:64]
    new_col = beta_two * cf[...] + (1.0 - beta_two) * (col_sum / 2048.0)
    ocf[...] = new_col
    each(lambda p: tot_copy(p).wait_recv())
    all_rows = jnp.sum(s.totr[...], axis=0)[0:4]
    row_mean = jnp.sum(all_rows, axis=1, keepdims=True) / 2048.0
    for w in range(4):
        col_wide = jnp.transpose(jnp.broadcast_to(new_col[w : w + 1, :], (128, 64)))
        second = new_row[w : w + 1, :] * col_wide / row_mean[w : w + 1, :]
        update = learn_rate * s.grad[w] * lax.rsqrt(second)
        ow[w] = wts[w] - jnp.transpose(update)

    each(lambda p: row_copy(p).wait_send())
    each(lambda p: col_copy(p).wait_send())
    each(lambda p: tot_copy(p).wait_send())
    for copy, cond in to_finish:
        if cond is None:
            copy.wait_send()
        else:
            @pl.when(cond)
            def _(copy=copy):
                copy.wait_send()


def body(
    layer_input, queries, key_rows, value_rows, context, grad_context, grad_output, earlier_mass,
    grad_queries, grad_keys, grad_values, documents, weights, row_factor, column_factor,
):
    far = pl.BlockSpec(memory_space=pl.ANY)
    near = pl.BlockSpec(memory_space=pltpu.VMEM)
    return pl.pallas_call(
        kernel,
        out_shape=(
            jax.ShapeDtypeStruct((4, 128, 64), full),
            jax.ShapeDtypeStruct((4, 128), full),
            jax.ShapeDtypeStruct((4, 64), full),
        ),
        in_specs=[far] * 7 + [near] + [far] * 3 + [near] * 4,
        out_specs=(near, near, near),
        scratch_shapes=list(SCRATCH.values()),
        compiler_params=pltpu.CompilerParams(
            collective_id=0, has_side_effects=True, vmem_limit_bytes=60 * 1024 * 1024
        ),
    )(
        layer_input[0], queries[0], key_rows[0], value_rows[0], context[0], grad_context[0],
        grad_output[0], earlier_mass[0], grad_queries[0], grad_keys[0], grad_values[0], documents,
        weights, row_factor, column_factor,
    )


def solution(mesh):
    placed = (P("dp", "blk", None),) * 7 + (P("dp", None, "blk"),) + (P("dp", "blk", None),) * 3 + (
        P("dp", "blk"),
        P(None, "blk", "dp"),
        P(None, "blk"),
        P(None, "dp"),
    )
    return jax.shard_map(
        body,
        mesh=mesh,
        in_specs=placed,
        out_specs=(P(None, "blk", "dp"), P(None, "blk"), P(None, "dp")),
        check_vma=False,
    )
```

time: 403 us -> 139 us (0.34)
  waiting for transfers between devices: 262 us -> 0 us
  Pallas kernels: 0 us -> 133 us
  blocking collectives: 47.8 us -> 0 us
  starting transfers between devices: 27.7 us -> 0 us
  other arithmetic: 19.2 us -> 0 us
  matrix products: 14 us -> 0 us
  between operations: 14.4 us -> 0.65 us
  local copies, waits for them, and re-layouts: 16.6 us -> 4.71 us
    reduce_scatter x1 -> x0, waiting for transfers between devices: 181 us -> none  [body(): lax.psum_scatter(jnp.concatenate([part_inner, part_output[:, None, :]], a...]
    pallas_call x0 -> x1, Pallas kernels: none -> 133 us  [body(): pl.pallas_call(kernel, out_shape=(jax.ShapeDtypeStruct((4, 128, 64), full...]
    ppermute x10 -> x0, waiting for transfers between devices: 68.1 us -> none  [passed_along(): return lax.ppermute(value, axis, pairs)]
    all_to_all x2 -> x0, blocking collectives: 47.8 us -> none  [the longest x1 34.3 us: sum_at_owner(): lax.all_to_all(in_blocks(array, dim, devices), axis, 0, 0, tiled=True)]
    ppermute x10 -> x0, starting transfers between devices: 19.8 us -> none  [passed_along(): return lax.ppermute(value, axis, pairs)]
    concatenate x4 -> x0, other arithmetic: 14.6 us -> none  [the longest x1 12.2 us: body(): jnp.concatenate([part_inner, part_output[:, None, :]], axis=1)]
    dot_general x7 -> x0, matrix products: 14 us -> none  [the longest x1 6.36 us: body(): jnp.einsum('twh,td->hwd', right_low, layer_rows, preferred_element_type=j...]
    all_to_all x2 -> x0, waiting for transfers between devices: 13.2 us -> none  [from_everyone(): lax.all_to_all(jnp.broadcast_to(array[None], (devices, *array.shape)), ax...]
  transfers between devices with their start and end apart: 13 -> 0, of which waited for: 10 -> 0; matrix products, arithmetic and copies ran while one was open for 6% -> 0% of each run, Pallas kernels for 0% -> 0%
where the time goes in v1:
time: 139 us
  Pallas kernels  133 us (96%)
  local copies, waits for them, and re-layouts  4.71 us (3%)
    pallas_call x1, Pallas kernels, body(): pl.pallas_call(kernel, out_shape=(jax.ShapeDtypeStruct((4, 128, 64), full...  133 us
    unnamed x7, local copies, waits for them, and re-layouts  2.99 us

profile of v1, /device:TPU:1, one launch (start us, length us, event | category | flops | bytes accessed | tf_op | source)
XLA Modules:
  0.0 138.8 jit_solution(11990637300561822138)
XLA Ops:
  0.6 1.7 %copy.18.wts = f32[4,128,64]{2,1,0:T(8,128)} copy(f32[4,128,64]{1,2,0:T(8,128)} %param.27) | data formatting | bytes 262144 | tf_op args[12]
  2.4 133.4 %shard_map.166 = (f32[4,128,64]{2,1,0:T(8,128)}, f32[4,128]{1,0:T(4,128)}, f32[4,64]{1,0:T(4,128)}) custom-call(bf16[256,2048]{1,0:T(8,128)(2,1)} %bitcast.11, bf16[256,1024]{1,0:T(8,128)(2,1)} %bitcast.16, bf16[256,1024]{1,0:T(8,128)(2,1)} %bitcast.17, bf16[256,1024]{1,0:T(8,128)(2,1)} %bitcast.18, bf16[256,1024]{1,0:T(8,128)(2,1)} %bitcast.19, ...), custom_call_target="tpu_custom_call" | custom-call | tf_op jit(solution)/shard_map/pallas_call | solution.py:565
  135.8 0.0 copy-start.1
  135.8 1.7 %copy.19 = f32[4,128,64]{1,2,0:T(8,128)} copy(f32[4,128,64]{2,1,0:T(8,128)} %get-tuple-element.3) | data formatting | bytes 262144 | tf_op jit(solution)/shard_map/pallas_call | solution.py:565
  137.5 0.0 copy-done.1
  137.5 0.0 copy-start
  137.5 0.6 copy.22
  138.1 0.1 copy-done
  138.2 0.6 copy.23
Async XLA Ops:
  135.8 1.7 %copy-start.1 = (f32[4,128]{1,0:T(4,128)S(1)}, f32[4,128]{1,0:T(4,128)}, u32[]{:S(2)}) copy-start(f32[4,128]{1,0:T(4,128)} %get-tuple-element.10) | copy-start | bytes 6148
  137.5 0.7 copy-start

commit v2 on v1

--- a/solution.py
+++ b/solution.py
@@ -24,13 +24,13 @@
     return lax.dot_general(a, b, dims, preferred_element_type=full)
 
 
-def group_scratch(tag, w):
+def group_scratch(tag, w, lanes):
     return {
-        "p_" + tag: pltpu.VMEM((4, 2, 4, w, 64, 512), low),
-        "xa_" + tag: pltpu.VMEM((2, 2, w, 64, 512), low),
-        "xb_" + tag: pltpu.VMEM((2, 4, w, 64, 512), low),
-        "ya_" + tag: pltpu.VMEM((2, w, 32, 512), low),
-        "yb_" + tag: pltpu.VMEM((2, w, 64, 512), low),
+        "p_" + tag: pltpu.VMEM((4, 1024 // lanes, 4, w, 64, lanes), low),
+        "xa_" + tag: pltpu.VMEM((2, 2, w, 64, lanes), low),
+        "xb_" + tag: pltpu.VMEM((2, 4, w, 64, lanes), low),
+        "ya_" + tag: pltpu.VMEM((2, w, 32, lanes), low),
+        "yb_" + tag: pltpu.VMEM((2, w, 64, lanes), low),
         "ea_" + tag: pltpu.VMEM((4, 2, w, 32, 512), low),
         "eb_" + tag: pltpu.VMEM((4, 2, w, 64, 512), low),
         "fa_" + tag: pltpu.VMEM((2, w, 32, 512), low),
@@ -42,7 +42,7 @@
     }
 
 
-N_SEM = 160
+N_SEM = 240
 SCRATCH = {
     "ly": pltpu.VMEM((2, 256, 2048), low),
     "gt": pltpu.VMEM((2, 256, 2048), low),
@@ -75,8 +75,10 @@
     "colr": pltpu.VMEM((16, 8, 128), full),
     "totr": pltpu.VMEM((16, 8, 128), full),
     "grad": pltpu.VMEM((4, 64, 128), full),
-    **group_scratch("o", 1),
-    **group_scratch("m", 3),
+    "z_send": pltpu.SemaphoreType.DMA((2, 8)),
+    "z_recv": pltpu.SemaphoreType.DMA((2, 8)),
+    **group_scratch("o", 1, 1024),
+    **group_scratch("m", 3, 512),
     "send": pltpu.SemaphoreType.DMA((N_SEM,)),
     "recv": pltpu.SemaphoreType.DMA((N_SEM,)),
     "local": pltpu.SemaphoreType.DMA((40,)),
@@ -214,20 +216,24 @@
     go_docs = remote(s.ds, s.dr, dn_b)
     send_rto = remote(s.rtf_o.at[:, :, :, 1 - c], s.rtp_o, mate)
     send_gt = remote(gout, s.gt.at[1], mate)
-    forward = []
-    for i in range(4):
-        forward.append(
-            [
-                (remote(k.at[lower, cols[i]], s.kk.at[i, pl.ds(256, 128)], dn_b), None),
-                (remote(q.at[upper, cols[i]], s.qr.at[i, 0], up_b), None),
-                (remote(k.at[upper, cols[i]], s.kk.at[i, pl.ds(384, 128)], dn_b, sends_up_k), plain),
-                (remote(q.at[lower, cols[i]], s.qr.at[i, 1], up_b, sends_low_q), wrapped),
-                (remote(v.at[lower, cols[i]], s.vv.at[i, pl.ds(256, 128)], dn_b), None),
-                (remote(go.at[upper, cols[i]], s.orr.at[i, 0], up_b), None),
-                (remote(v.at[upper, cols[i]], s.vv.at[i, pl.ds(384, 128)], dn_b, sends_up_k), plain),
-                (remote(go.at[lower, cols[i]], s.orr.at[i, 1], up_b, sends_low_q), wrapped),
-            ]
-        )
+    forward = {}
+
+    def send_forward(i):
+        k_low = remote(k.at[lower, cols[i]], s.kk.at[i, pl.ds(256, 128)], dn_b)
+        q_up = remote(q.at[upper, cols[i]], s.qr.at[i, 0], up_b)
+        k_up = remote(k.at[upper, cols[i]], s.kk.at[i, pl.ds(384, 128)], dn_b, sends_up_k)
+        q_low = remote(q.at[lower, cols[i]], s.qr.at[i, 1], up_b, sends_low_q)
+        v_low = remote(v.at[lower, cols[i]], s.vv.at[i, pl.ds(256, 128)], dn_b)
+        o_up = remote(go.at[upper, cols[i]], s.orr.at[i, 0], up_b)
+        v_up = remote(v.at[upper, cols[i]], s.vv.at[i, pl.ds(384, 128)], dn_b, sends_up_k)
+        o_low = remote(go.at[lower, cols[i]], s.orr.at[i, 1], up_b, sends_low_q)
+        forward[i] = [
+            (k_low, None), (q_up, None), (k_up, plain), (q_low, wrapped),
+            (v_low, None), (o_up, None), (v_up, plain), (o_low, wrapped),
+        ]
+
+    send_forward(0)
+    send_forward(1)
     send_ly = remote(lay, s.ly.at[1], mate)
 
     def weight_part(left, mate_left, right, p_ref, i, w):
@@ -236,8 +242,9 @@
             out = dot(left, right[0, :, lanes], NN) + dot(mate_left, right[1, :, lanes], NN)
             out = out.astype(low).reshape(-1, w, 2, 64, 256)
             y_hi = lax.div(db, 4)
-            half = lax.rem(lax.div(db, 2), 2)
-            at_lane = pl.ds(pl.multiple_of(lax.rem(db, 2) * 256, 256), 256)
+            per_half = p_ref.shape[-1] // 256
+            half = lax.div(lax.rem(db, 4), per_half)
+            at_lane = pl.ds(pl.multiple_of(lax.rem(db, per_half) * 256, 256), 256)
             for n in range(out.shape[0]):
                 for one in range(2):
                     p_ref[i + n, half, y_hi * 2 + one, :, :, at_lane] = out[n, :, one]
@@ -258,7 +265,8 @@
             self.w = w
             for name in ("p", "xa", "xb", "ya", "yb", "ea", "eb", "fa", "fb", "zs", "zr", "rtf", "rtp"):
                 setattr(self, name, getattr(s, name + "_" + tag))
-            self.ea_copy, self.eb_copy = {}, {}
+            self.ea_copy, self.eb_copy, self.xb_copy = {}, {}, {}
+            self.index = 0 if tag == "o" else 1
 
         def x_first(self, i):
             p = self.p
@@ -268,25 +276,36 @@
             elif i == 1:
                 arrived(self.xa0)
                 add_to(p.at[1, 0, pl.ds(0, 2)], self.xa.at[0])
-                self.xb0 = remote(p.at[1, 0], self.xb.at[0], up_x)
+                self.send_chunks(1, 0, up_x)
             elif i == 2:
                 arrived(self.xa1)
                 add_to(p.at[2, 0, pl.ds(2, 2)], self.xa.at[1])
-                self.xb1 = remote(p.at[2, 0], self.xb.at[1], dn_x)
+                self.send_chunks(2, 1, dn_x)
+
+        def send_chunks(self, i, way, device):
+            self.xb_copy[way] = [
+                remote(self.p.at[i, 0, chunk], self.xb.at[way, chunk], device)
+                for chunk in (y_two, y_one, y_three, y)
+            ]
+
+        def take_chunk(self, n, chunk):
+            arrived(self.xb_copy[0][n])
+            arrived(self.xb_copy[1][n])
+            return (self.xb.at[0, chunk], self.xb.at[1, chunk])
 
         def x_first_end(self):
             p = self.p
-            arrived(self.xb0)
-            arrived(self.xb1)
-            add_to(p.at[3, 0], self.xb.at[0], self.xb.at[1])
+            add_to(p.at[3, 0, y_two], *self.take_chunk(0, y_two))
             self.ya0 = remote(p.at[3, 0, y_two, :, top], self.ya.at[0], up_y)
             self.ya1 = remote(p.at[3, 0, y_two, :, bottom], self.ya.at[1], dn_y)
 
         def then_y(self):
             p = self.p
+            add_to(p.at[3, 0, y_one], *self.take_chunk(1, y_one))
             arrived(self.ya0)
             add_to(p.at[3, 0, y_one, :, top], self.ya.at[0])
             self.yb0 = remote(p.at[3, 0, y_one], self.yb.at[0], up_y)
+            add_to(p.at[3, 0, y_three], *self.take_chunk(2, y_three))
             arrived(self.ya1)
             add_to(p.at[3, 0, y_three, :, bottom], self.ya.at[1])
             self.yb1 = remote(p.at[3, 0, y_three], self.yb.at[1], dn_y)
@@ -325,31 +344,48 @@
                 add_to(p.at[2, 1, y, :, bottom], self.fa.at[1])
                 self.fb1 = remote(mine, self.fb.at[1], dn_x)
 
-        def stage(self, mine, one, two, base):
-            total = mine[...].astype(full) + one[...].astype(full) + two[...].astype(full)
+        def stage(self, mine, others, base):
+            total = mine[...].astype(full)
+            for other in others:
+                total = total + other[...].astype(full)
             total = total.astype(low)
-            for n in range(4):
+            pieces = total.shape[-1] // 128
+            for n in range(pieces):
                 self.zs[base + n] = total[:, :, n * 128 : (n + 1) * 128]
-
-        def along_z(self):
+            for there in range(base, base + pieces):
+                @pl.when(z != there)
+                def _():
+                    self.z_copy(there, lax.rem(there - z + 8, 8)).start()
+
+        def z_copy(self, there, p):
+            return pltpu.make_async_remote_copy(
+                src_ref=self.zs.at[there], dst_ref=self.zr.at[p],
+                send_sem=s.z_send.at[self.index, p], recv_sem=s.z_recv.at[self.index, p],
+                device_id=at(x, y, there), device_id_type=pl.DeviceIdType.MESH,
+            )
+
+        def second_along_z(self):
+            arrived(self.fb0)
+            arrived(self.fb1)
+            self.stage(self.p.at[3, 1, y], (self.fb.at[0], self.fb.at[1]), 4)
+
+        def first_along_z(self):
+            chunks = self.take_chunk(3, y)
             arrived(self.yb0)
             arrived(self.yb1)
-            self.stage(self.p.at[3, 0, y], self.yb.at[0], self.yb.at[1], 0)
-            arrived(self.fb0)
-            arrived(self.fb1)
-            self.stage(self.p.at[3, 1, y], self.fb.at[0], self.fb.at[1], 4)
-            self.z_copies = []
-            for p in (4, 3, 5, 2, 6, 1, 7):
-                there = lax.rem(z + p, 8)
-                self.z_copies.append(remote(self.zs.at[there], self.zr.at[p], at(x, y, there)))
+            self.stage(self.p.at[3, 0, y], chunks + (self.yb.at[0], self.yb.at[1]), 0)
 
         def total(self):
-            for copy in self.z_copies:
-                arrived(copy)
+            for p in range(1, 8):
+                self.z_copy(lax.rem(z + p, 8), p).wait_recv()
             total = self.zs[z].astype(full)
             for p in range(1, 8):
                 total = total + self.zr[p].astype(full)
             return total
+
+        def finish(self):
+            for p in range(1, 8):
+                self.z_copy(lax.rem(z + p, 8), p).wait_send()
 
     out_g, main_g = Group("o", 1), Group("m", 3)
 
@@ -360,8 +396,6 @@
         s.rtf_o[:, :, :, c].reshape(512, 256), s.rtp_o[...].reshape(512, 256), s.gt, s.p_o, 0, 1
     )
     out_g.x_first(0)
-    for i in range(4):
-        out_g.y_first(i)
 
     j = lax.rem(b + 15, 16)
     halves_here = jnp.where(wrapped, 2, 1)
@@ -410,13 +444,15 @@
         lax.fori_loop(0, halves_here, one_half, 0)
         s.dks[i] = s.acck[...].astype(low)
         s.dvs[i] = s.accv[...].astype(low)
+        q_up = remote(s.dqs.at[i, 0], s.dqr.at[i, 0], dn_b)
+        q_low = remote(s.dqs.at[i, 1], s.dqr.at[i, 1], dn_b, wrapped)
+        k_low = remote(s.dks.at[i, lower], s.dkr.at[i, lower], up_b)
+        k_up = remote(s.dks.at[i, upper], s.dkr.at[i, upper], up_b, plain)
+        v_low = remote(s.dvs.at[i, lower], s.dvr.at[i, lower], up_b)
+        v_up = remote(s.dvs.at[i, upper], s.dvr.at[i, upper], up_b, plain)
         returns[i] = [
-            (remote(s.dqs.at[i, 0], s.dqr.at[i, 0], dn_b), None),
-            (remote(s.dqs.at[i, 1], s.dqr.at[i, 1], dn_b, wrapped), sends_low_q),
-            (remote(s.dks.at[i, lower], s.dkr.at[i, lower], up_b), None),
-            (remote(s.dks.at[i, upper], s.dkr.at[i, upper], up_b, plain), sends_up_k),
-            (remote(s.dvs.at[i, lower], s.dvr.at[i, lower], up_b), None),
-            (remote(s.dvs.at[i, upper], s.dvr.at[i, upper], up_b, plain), sends_up_k),
+            (q_up, None), (q_low, sends_low_q), (k_low, None),
+            (k_up, sends_up_k), (v_low, None), (v_up, sends_up_k),
         ]
 
     exchanged = {}
@@ -453,40 +489,38 @@
     arrived(go_docs)
     s.dk[pl.ds(256, 256), :] = jnp.transpose(jnp.broadcast_to(s.dr[0:1, :], (128, 256)))
     attention(0)
+    send_forward(2)
     out_g.x_first(1)
     out_g.x_first(2)
-    for i in range(4):
-        out_g.y_second(i)
     attention(1)
+    send_forward(3)
     finalize(0)
-    for i in range(3):
-        out_g.y_end_then_x(i)
     out_g.x_first_end()
     load_ly.wait()
     arrived(send_ly)
+    attention(2)
     weights_of(0)
-    attention(2)
     finalize(1)
-    main_g.y_second(0)
-    weights_of(1)
-    out_g.y_end_then_x(3)
     out_g.then_y()
     attention(3)
+    weights_of(1)
+    main_g.y_second(0)
     finalize(2)
+    out_g.first_along_z()
+    weights_of(2)
     main_g.y_end_then_x(0)
     main_g.y_second(1)
-    weights_of(2)
-    out_g.along_z()
     finalize(3)
     main_g.y_end_then_x(1)
+    weights_of(3)
     main_g.y_second(2)
-    weights_of(3)
+    main_g.x_first_end()
     main_g.y_end_then_x(2)
-    main_g.x_first_end()
     main_g.y_second(3)
     main_g.then_y()
     main_g.y_end_then_x(3)
-    main_g.along_z()
+    main_g.second_along_z()
+    main_g.first_along_z()
     s.grad[3] = out_g.total()[0] * (1.0 / ALL_TOKENS)
     s.grad[pl.ds(0, 3)] = main_g.total() * (1.0 / ALL_TOKENS)
 
@@ -541,9 +575,10 @@
     for w in range(4):
         col_wide = jnp.transpose(jnp.broadcast_to(new_col[w : w + 1, :], (128, 64)))
         second = new_row[w : w + 1, :] * col_wide / row_mean[w : w + 1, :]
-        update = learn_rate * s.grad[w] * lax.rsqrt(second)
-        ow[w] = wts[w] - jnp.transpose(update)
-
+        ow[w] = wts[w] - learn_rate * s.grad[w] * lax.rsqrt(second)
+
+    out_g.finish()
+    main_g.finish()
     each(lambda p: row_copy(p).wait_send())
     each(lambda p: col_copy(p).wait_send())
     each(lambda p: tot_copy(p).wait_send())
@@ -562,10 +597,10 @@
 ):
     far = pl.BlockSpec(memory_space=pl.ANY)
     near = pl.BlockSpec(memory_space=pltpu.VMEM)
-    return pl.pallas_call(
+    new_weights, new_row, new_col = pl.pallas_call(
         kernel,
         out_shape=(
-            jax.ShapeDtypeStruct((4, 128, 64), full),
+            jax.ShapeDtypeStruct((4, 64, 128), full),
             jax.ShapeDtypeStruct((4, 128), full),
             jax.ShapeDtypeStruct((4, 64), full),
         ),
@@ -578,8 +613,9 @@
     )(
         layer_input[0], queries[0], key_rows[0], value_rows[0], context[0], grad_context[0],
         grad_output[0], earlier_mass[0], grad_queries[0], grad_keys[0], grad_values[0], documents,
-        weights, row_factor, column_factor,
+        jnp.transpose(weights, (0, 2, 1)), row_factor, column_factor,
     )
+    return jnp.transpose(new_weights, (0, 2, 1)), new_row, new_col
 
 
 def solution(mesh):

time: 139 us -> 123 us (0.88)
  Pallas kernels: 133 us -> 119 us
  local copies, waits for them, and re-layouts: 4.71 us -> 2.82 us
    pallas_call x1, Pallas kernels: 133 us -> 119 us  [body(): pl.pallas_call(kernel, out_shape=(jax.ShapeDtypeStruct((4, 64, 128), full...]
    pallas_call x1 -> x0, local copies, waits for them, and re-layouts: 1.72 us -> none  [body(): pl.pallas_call(kernel, out_shape=(jax.ShapeDtypeStruct((4, 128, 64), full...]
where the time goes in v2:
time: 123 us
  Pallas kernels  119 us (97%)
  local copies, waits for them, and re-layouts  2.82 us (2%)
    pallas_call x1, Pallas kernels, body(): pl.pallas_call(kernel, out_shape=(jax.ShapeDtypeStruct((4, 64, 128), full...  119 us
    unnamed x7, local copies, waits for them, and re-layouts  2.82 us

profile of v2, /device:TPU:1, one launch (start us, length us, event | category | flops | bytes accessed | tf_op | source)
XLA Modules:
  0.0 122.8 jit_solution(3513965665559646081)
XLA Ops:
  0.6 119.3 %shard_map.166 = (f32[4,64,128]{2,1,0:T(8,128)}, f32[4,128]{1,0:T(4,128)}, f32[4,64]{1,0:T(4,128)}) custom-call(bf16[256,2048]{1,0:T(8,128)(2,1)} %bitcast.13, bf16[256,1024]{1,0:T(8,128)(2,1)} %bitcast.18, bf16[256,1024]{1,0:T(8,128)(2,1)} %bitcast.19, bf16[256,1024]{1,0:T(8,128)(2,1)} %bitcast.20, bf16[256,1024]{1,0:T(8,128)(2,1)} %bitcast.21, ...), custom_call_target="tpu_custom_call" | custom-call | tf_op jit(solution)/shard_map/pallas_call | solution.py:600
  119.9 0.0 copy-start.1
  119.9 1.6 %copy.21 = f32[4,128,64]{1,2,0:T(8,128)} copy(f32[4,128,64]{1,2,0:T(8,128)} %bitcast.24) | data formatting | bytes 262144
  121.5 0.0 copy-done.1
  121.5 0.0 copy-start
  121.5 0.6 copy.22
  122.1 0.1 copy-done
  122.2 0.6 copy.23
Async XLA Ops:
  119.9 1.6 %copy-start.1 = (f32[4,128]{1,0:T(4,128)S(1)}, f32[4,128]{1,0:T(4,128)}, u32[]{:S(2)}) copy-start(f32[4,128]{1,0:T(4,128)} %get-tuple-element.13) | copy-start | bytes 6148
  121.5 0.7 copy-start

commit v3 on v2

--- a/solution.py
+++ b/solution.py
@@ -483,7 +483,8 @@
             s.rtf_m[i, :, :, c].reshape(384, 256), s.rtp_m[i].reshape(384, 256), s.ly, s.p_m, i, 3
         )
         main_g.x_first(i)
-        main_g.y_first(i)
+        if i > 1:
+            main_g.y_first(i)
 
     arrived(go_meta)
     arrived(go_docs)
@@ -495,24 +496,26 @@
     attention(1)
     send_forward(3)
     finalize(0)
-    out_g.x_first_end()
     load_ly.wait()
     arrived(send_ly)
     attention(2)
     weights_of(0)
     finalize(1)
-    out_g.then_y()
+    out_g.x_first_end()
     attention(3)
     weights_of(1)
+    finalize(2)
+    main_g.y_first(0)
+    main_g.y_first(1)
+    out_g.then_y()
+    weights_of(2)
     main_g.y_second(0)
-    finalize(2)
-    out_g.first_along_z()
-    weights_of(2)
-    main_g.y_end_then_x(0)
     main_g.y_second(1)
     finalize(3)
+    main_g.y_end_then_x(0)
+    weights_of(3)
     main_g.y_end_then_x(1)
-    weights_of(3)
+    out_g.first_along_z()
     main_g.y_second(2)
     main_g.x_first_end()
     main_g.y_end_then_x(2)

time: 123 us -> 117 us (0.951)
  Pallas kernels: 119 us -> 114 us
    pallas_call x1, Pallas kernels: 119 us -> 114 us  [body(): pl.pallas_call(kernel, out_shape=(jax.ShapeDtypeStruct((4, 64, 128), full...]
where the time goes in v3:
time: 117 us
  Pallas kernels  114 us (97%)
  local copies, waits for them, and re-layouts  2.82 us (2%)
    pallas_call x1, Pallas kernels, body(): pl.pallas_call(kernel, out_shape=(jax.ShapeDtypeStruct((4, 64, 128), full...  114 us
    unnamed x7, local copies, waits for them, and re-layouts  2.82 us

profile of v3, /device:TPU:1, one launch (start us, length us, event | category | flops | bytes accessed | tf_op | source)
XLA Modules:
  0.0 117.2 jit_solution(8624489447816721447)
XLA Ops:
  0.6 113.7 %shard_map.166 = (f32[4,64,128]{2,1,0:T(8,128)}, f32[4,128]{1,0:T(4,128)}, f32[4,64]{1,0:T(4,128)}) custom-call(bf16[256,2048]{1,0:T(8,128)(2,1)} %bitcast.13, bf16[256,1024]{1,0:T(8,128)(2,1)} %bitcast.18, bf16[256,1024]{1,0:T(8,128)(2,1)} %bitcast.19, bf16[256,1024]{1,0:T(8,128)(2,1)} %bitcast.20, bf16[256,1024]{1,0:T(8,128)(2,1)} %bitcast.21, ...), custom_call_target="tpu_custom_call" | custom-call | tf_op jit(solution)/shard_map/pallas_call | solution.py:603
  114.4 0.0 copy-start.1
  114.4 1.6 %copy.21 = f32[4,128,64]{1,2,0:T(8,128)} copy(f32[4,128,64]{1,2,0:T(8,128)} %bitcast.24) | data formatting | bytes 262144
  115.9 0.0 copy-done.1
  115.9 0.0 copy-start
  115.9 0.6 copy.22
  116.5 0.1 copy-done
  116.6 0.6 copy.23
Async XLA Ops:
  114.4 1.6 %copy-start.1 = (f32[4,128]{1,0:T(4,128)S(1)}, f32[4,128]{1,0:T(4,128)}, u32[]{:S(2)}) copy-start(f32[4,128]{1,0:T(4,128)} %get-tuple-element.13) | copy-start | bytes 6148
  115.9 0.7 copy-start
